TPU v7x, 8 devices: a whole 2x2x1 slice. The times are simulated.
8 devices in a mesh: dp: 1 (over z), tp: 2 (over y), kvp: 4 (over x, core).
Axes of the slice: x: 2, y: 2, z: 1, core: 2. Of those that a mesh axis runs over, the one named last changes fastest.
Arguments:
- x_in: bfloat16 [32, 3072], P('dp')
- ctx_len: int32 [32], P('dp')
- g_attn: bfloat16 [3072], replicated
- g_mlp: bfloat16 [3072], replicated
- w_qkv: bfloat16 [3072, 5120], P(None, 'tp')
- w_o: bfloat16 [3072, 3072], P(('tp', 'kvp'))
- w_gate: bfloat16 [3072, 8192], P(None, ('tp', 'kvp'))
- w_up: bfloat16 [3072, 8192], P(None, ('tp', 'kvp'))
- w_down: bfloat16 [8192, 3072], P(('tp', 'kvp'))
- k_cache: bfloat16 [32, 1024, 8, 128], P('dp', 'kvp', 'tp')
- v_cache: bfloat16 [32, 1024, 8, 128], P('dp', 'kvp', 'tp')
Outputs:
- output 1: bfloat16 [32, 3072], P('dp')
- output 2: bfloat16 [32, 1024, 8, 128], P('dp', 'kvp', 'tp')
- output 3: bfloat16 [32, 1024, 8, 128], P('dp', 'kvp', 'tp')
All inputs are finite; a program needn't handle non-finite values.
Results may differ from a plain program's by a relative error of at most 0.00825897.
Values sent between devices are 32-bit elements.
A program may use at most 1 GiB of HBM per device.

v0:
```python
import jax
import jax.numpy as jnp
from jax import lax
from jax.sharding import PartitionSpec as P

ROPE_THETA = 500000.0
EPS = 1e-5
NEG_FILL = -1e30


def rms_norm(values, gain_vec):
    x_f32 = values.astype(jnp.float32)
    inv_rms = lax.rsqrt(jnp.mean(x_f32 * x_f32, axis=-1, keepdims=True) + EPS)
    return (x_f32 * inv_rms * gain_vec.astype(jnp.float32)).astype(jnp.bfloat16)


def rope_tables(ctx_len, head_dim):
    inv_freq = ROPE_THETA ** (-2.0 * jnp.arange(head_dim // 2, dtype=jnp.float32) / head_dim)
    angles = ctx_len.astype(jnp.float32)[:, None] * inv_freq[None, :]
    return jnp.cos(angles), jnp.sin(angles)


def rotary(vectors, cos_t, sin_t):
    half_dim = vectors.shape[-1] // 2
    first_half = vectors[..., :half_dim]
    second_half = vectors[..., half_dim:]
    return jnp.concatenate([first_half * cos_t - second_half * sin_t, second_half * cos_t + first_half * sin_t], axis=-1)


def mlp_part(hidden, g_mlp, w_gate, w_up, w_down):
    normed = rms_norm(hidden, g_mlp)
    gate_pre = jnp.dot(normed, w_gate, preferred_element_type=jnp.float32)
    up_proj = jnp.dot(normed, w_up, preferred_element_type=jnp.float32)
    act_out = (jax.nn.silu(gate_pre) * up_proj).astype(jnp.bfloat16)
    return jnp.dot(act_out, w_down, preferred_element_type=jnp.float32)


def local_attention(x_in, ctx_len, g_attn, w_qkv, k_cache, v_cache, kvp_index):
    batch_rows, block_len, kv_local, head_dim = k_cache.shape
    group_size = w_qkv.shape[1] // (kv_local * head_dim) - 2
    normed = rms_norm(x_in, g_attn)
    qkv_all = jnp.dot(normed, w_qkv, preferred_element_type=jnp.float32).reshape(batch_rows, kv_local, group_size + 2, head_dim)
    cos_t, sin_t = rope_tables(ctx_len, head_dim)
    queries = rotary(qkv_all[:, :, :group_size], cos_t[:, None, None, :], sin_t[:, None, None, :]).astype(jnp.bfloat16)
    key_new = rotary(qkv_all[:, :, group_size], cos_t[:, None, :], sin_t[:, None, :]).astype(jnp.bfloat16)
    val_new = qkv_all[:, :, group_size + 1].astype(jnp.bfloat16)
    positions = kvp_index * block_len + jnp.arange(block_len)
    hit_mask = (positions[None, :] == ctx_len[:, None])[:, :, None, None]
    k_out = jnp.where(hit_mask, key_new[:, None], k_cache)
    v_out = jnp.where(hit_mask, val_new[:, None], v_cache)
    scores = jnp.einsum("bgrd,btgd->bgrt", queries, k_out, preferred_element_type=jnp.float32) * head_dim ** -0.5
    valid = (positions[None, :] <= ctx_len[:, None])[:, None, None, :]
    scores = jnp.where(valid, scores, NEG_FILL)
    local_max = jnp.max(scores, axis=-1)
    prob_w = jnp.exp(scores - local_max[..., None])
    local_sum = jnp.sum(prob_w, axis=-1)
    local_acc = jnp.einsum("bgrt,btgd->bgrd", prob_w.astype(jnp.bfloat16), v_out, preferred_element_type=jnp.float32)
    return local_max, local_sum, local_acc, k_out, v_out


def solution(mesh):
    x_spec = P("dp", None)
    cache_spec = P("dp", "kvp", "tp", None)
    model_axes = ("tp", "kvp")

    def layer_step(x_in, ctx_len, g_attn, g_mlp, w_qkv, w_o, w_gate, w_up, w_down, k_cache, v_cache):
        kvp_index = lax.axis_index("kvp")
        local_max, local_sum, local_acc, k_out, v_out = local_attention(x_in, ctx_len, g_attn, w_qkv, k_cache, v_cache, kvp_index)
        batch_rows = local_acc.shape[0]
        attn_width = local_acc.shape[1] * local_acc.shape[2] * local_acc.shape[3]
        rows_own = w_o.shape[0]
        global_max = lax.pmax(local_max, "kvp")
        rescale = jnp.exp(local_max - global_max)
        denom_sum = lax.psum(local_sum * rescale, "kvp")
        acc_part = (local_acc * rescale[..., None]).reshape(batch_rows, attn_width)
        acc_own = lax.psum_scatter(acc_part, "kvp", scatter_dimension=1, tiled=True)
        denom_rows = jnp.broadcast_to(denom_sum[..., None], local_acc.shape).reshape(batch_rows, attn_width)
        denom_own = lax.dynamic_slice_in_dim(denom_rows, kvp_index * rows_own, rows_own, axis=1)
        attn_own = (acc_own / denom_own).astype(jnp.bfloat16)
        attn_sum = lax.psum(jnp.dot(attn_own, w_o, preferred_element_type=jnp.float32), model_axes)
        hidden = (x_in.astype(jnp.float32) + attn_sum).astype(jnp.bfloat16)
        mlp_sum = lax.psum(mlp_part(hidden, g_mlp, w_gate, w_up, w_down), model_axes)
        x_out = (hidden.astype(jnp.float32) + mlp_sum).astype(jnp.bfloat16)
        return x_out, k_out, v_out

    in_specs = (x_spec, P("dp"), P(None), P(None), P(None, "tp"), P(model_axes, None), P(None, model_axes), P(None, model_axes), P(model_axes, None), cache_spec, cache_spec)
    return jax.shard_map(layer_step, mesh=mesh, in_specs=in_specs, out_specs=(x_spec, cache_spec, cache_spec), check_vma=False)
```

profile of v0, /device:TPU:0, one launch (start us, length us, event | category | flops | bytes accessed | tf_op | source)
XLA Modules:
  0.0 182.3 jit_solution(99910932229478028)
XLA Ops:
  7.2 0.8 convert_element_type.53
  8.1 1.1 fusion.17
  9.2 8.5 %fusion.27 = f32[32,2560]{1,0:T(8,128)S(1)} fusion(bf16[3072,2560]{1,0:T(8,128)(2,1)} %param.15, bf16[32,3072]{1,0:T(8,128)(2,1)} %param.11, f32[3072]{0:T(1024)S(1)} %convert_element_type.53, f32[32]{0:T(128)S(1)} %add_rsqrt_fusion.1), kind=kOutput, calls=%fused_computation.32 | convolution fusion | flops 503709696 | bytes 16265344 | tf_op jit(solution)/shard_map/dot_general | solution.py:42
  17.6 0.2 reshape.203
  18.1 0.1 multiply_cosine_fusion
  18.2 0.2 subtract_convert_fusion
  18.7 13.7 %broadcast_select_fusion.1 = (bf16[32,256,4,128]{3,2,1,0:T(4,128)(2,1)S(1)}, bf16[32,256,4,128]{3,2,1,0:T(4,128)(2,1)}) fusion(bf16[32,256,4,128]{3,2,1,0:T(4,128)(2,1)} %param.20, pred[32,256]{1,0:T(8,128)(4,1)S(1)} %get-tuple-element.14, bf16[32,4,128]{2,1,0:T(4,128)(2,1)S(1)} %pad_maximum_fusion, bf16[32,256,4,128]{3,2,1,0:T(4,128)(2,1)} %param.21, ...), kind=kLoop, calls=%fused_computation.5 | loop fusion | flops 8388608 | bytes 33628160 | tf_op jit(solution)/shard_map/jit(_where)/select_n | solution.py:49
  32.5 3.4 %copy-done.1 = bf16[32,256,4,128]{3,2,1,0:T(4,128)(2,1)} copy-done((bf16[32,256,4,128]{3,2,1,0:T(4,128)(2,1)}, bf16[32,256,4,128]{3,2,1,0:T(4,128)(2,1)S(1)}, u32[]{:S(2)}) %copy-start.1) | copy-done | bytes 8388632
  35.9 2.4 %fusion.50 = (f32[32,4,3]{2,1,0:T(4,128)S(1)}, f32[32,4,3,256]{3,2,1,0:T(4,128)S(1)}) fusion(bf16[32,256,4,128]{3,2,1,0:T(4,128)(2,1)S(1)} %get-tuple-element.11, bf16[32,4,3,64]{3,2,1,0:T(4,128)(2,1)S(1)} %get-tuple-element.8, bf16[32,4,3,64]{3,2,1,0:T(4,128)(2,1)S(1)} %get-tuple-element.7, pred[32,256]{1,0:T(8,128)(4,1)S(1)} %get-tuple-element.13), kind=kOutput, calls=%fused_computation.65 | convolution fusion | flops 25656960 | bytes 8889856 | tf_op jit(solution)/shard_map/bgrd,btgd->bgrt/dot_general | solution.py:51
  38.3 13.9 %pmax.7 = f32[32,4,3]{2,1,0:T(4,128)S(1)} all-reduce(f32[32,4,3]{2,1,0:T(4,128)S(1)} %get-tuple-element.17), channel_id=1, replica_groups=mesh['dp'=1,'tp'=2,'kvp'=4] {'kvp'}, use_global_device_ids=true, to_apply=%region_2.3 | all-reduce | flops 384 | bytes 3072 | tf_op jit(solution)/shard_map/pmax | solution.py:72
  52.2 0.5 fusion.15
  52.7 4.6 %fusion.7 = f32[32,4,3,128]{3,2,1,0:T(4,128)S(1)} fusion(bf16[32,256,4,128]{3,2,1,0:T(4,128)(2,1)} %get-tuple-element.12, f32[32,4,3,256]{3,2,1,0:T(4,128)S(1)} %get-tuple-element.18, f32[32,4,3]{2,1,0:T(4,128)S(1)} %get-tuple-element.17, f32[32,4,3]{2,1,0:T(4,128)S(1)} %bitcast.20), kind=kOutput, calls=%fused_computation.7 | convolution fusion | flops 25411584 | bytes 8981504 | tf_op jit(solution)/shard_map/bgrt,btgd->bgrd/dot_general | solution.py:57
  57.4 0.8 reshape.204
  58.2 10.7 %psum.21 = f32[32,4,3]{2,1,0:T(4,128)S(1)} all-reduce(f32[32,4,3]{2,1,0:T(4,128)S(1)} %bitcast.17), channel_id=1, replica_groups=mesh['dp'=1,'tp'=2,'kvp'=4] {'kvp'}, use_global_device_ids=true, to_apply=%region_5.6 | all-reduce | flops 384 | bytes 3072 | tf_op jit(solution)/shard_map/psum | solution.py:74
  69.0 0.2 broadcast_in_dim.43
  69.2 0.1 reshape.205
  69.3 3.3 %reduce-scatter.2.cloned.1.call-done = f32[32,384]{1,0:T(8,128)} async-done(((f32[32,1536]{1,0:T(8,128)}), f32[32,384]{1,0:T(8,128)}) %reduce-scatter.2.cloned.1.call-update) | async-done | bytes 49168 | tf_op jit(solution)/shard_map/reduce_scatter | solution.py:76
  72.6 2.1 %fusion.44 = f32[32,3072]{1,0:T(8,128)} fusion(bf16[384,3072]{1,0:T(8,128)(2,1)S(1)} %copy-done, f32[32,384]{1,0:T(8,128)} %reduce-scatter.2.cloned.1.call-done, f32[32,1536]{1,0:T(8,128)S(1)} %reshape.205, s32[]{:T(128)S(6)} %select_n.17), kind=kOutput, calls=%fused_computation.52 | convolution fusion | flops 75522048 | bytes 2850820 | tf_op jit(solution)/shard_map/dot_general | solution.py:80
  74.7 43.9 %all-reduce.3.cloned.1.call-done = f32[32,3072]{1,0:T(8,128)} async-done(((f32[32,3072]{1,0:T(8,128)}), f32[32,3072]{1,0:T(8,128)}) %all-reduce.3.cloned.1.call-update) | async-done | bytes 393232 | tf_op jit(solution)/shard_map/psum | solution.py:80
  118.7 1.2 fusion.21
  119.8 4.0 %fusion.42 = f32[32,1024]{1,0:T(8,128)S(1)} fusion(bf16[3072,1024]{1,0:T(8,128)(2,1)} %param.17, bf16[32,3072]{1,0:T(8,128)(2,1)S(1)} %get-tuple-element.4, f32[3072]{0:T(1024)S(1)} %convert_element_type.61, f32[32]{0:T(128)S(1)} %add_rsqrt_fusion), kind=kOutput, calls=%fused_computation.48 | convolution fusion | flops 201719808 | bytes 6631552 | tf_op jit(solution)/shard_map/dot_general | solution.py:32
  123.9 7.7 %fusion.14 = f32[32,3072]{1,0:T(8,128)} fusion(bf16[1024,3072]{1,0:T(8,128)(2,1)} %param.19, bf16[3072,1024]{1,0:T(8,128)(2,1)} %param.18, f32[32,1024]{1,0:T(8,128)S(1)} %fusion.42, bf16[32,3072]{1,0:T(8,128)(2,1)S(1)} %get-tuple-element.4, f32[3072]{0:T(1024)S(1)} %convert_element_type.61, f32[32]{0:T(128)S(1)} %add_rsqrt_fusion), kind=kOutput, calls=%fused_computation.11 | convolution fusion | flops 403243008 | bytes 13316224 | tf_op jit(solution)/shard_map/dot_general | solution.py:35
  131.6 42.4 %all-reduce.5.cloned.1.call-done = f32[32,3072]{1,0:T(8,128)} async-done(((f32[32,3072]{1,0:T(8,128)}), f32[32,3072]{1,0:T(8,128)}) %all-reduce.5.cloned.1.call-update) | async-done | bytes 393232 | tf_op jit(solution)/shard_map/psum | solution.py:82
  174.0 1.7 fusion.24
  (29 shorter events, 0.7 us)
Async XLA Ops:
  7.2 65.4 %copy-start = (bf16[384,3072]{1,0:T(8,128)(2,1)S(1)}, bf16[384,3072]{1,0:T(8,128)(2,1)}, u32[]{:S(2)}) copy-start(bf16[384,3072]{1,0:T(8,128)(2,1)} %param.16) | copy-start | bytes 7077892
  7.2 65.4 %reduce-scatter.2.cloned.1.call-start = ((), (), s32[]{:S(2)}) async-start(), calls=%async_computation.1 | async-start | bytes 245760 | tf_op jit(solution)/shard_map/reduce_scatter | solution.py:76
  9.2 8.8 %copy-start.4 = (s32[32]{0:T(128)S(1)}, s32[32]{0:T(128)}, u32[]{:S(2)}) copy-start(s32[32]{0:T(128)} %param.12) | copy-start | bytes 388
  32.5 3.4 %copy-start.1 = (bf16[32,256,4,128]{3,2,1,0:T(4,128)(2,1)}, bf16[32,256,4,128]{3,2,1,0:T(4,128)(2,1)S(1)}, u32[]{:S(2)}) copy-start(bf16[32,256,4,128]{3,2,1,0:T(4,128)(2,1)S(1)} %get-tuple-element.11) | copy-start | bytes 25165828
  38.3 36.5 %copy-start.3 = (bf16[3072]{0:T(1024)(128)(2,1)S(1)}, bf16[3072]{0:T(1024)(128)(2,1)}, u32[]{:S(2)}) copy-start(bf16[3072]{0:T(1024)(128)(2,1)} %param.14) | copy-start | bytes 18436
  38.3 80.4 %copy-start.2 = (bf16[32,3072]{1,0:T(8,128)(2,1)S(1)}, bf16[32,3072]{1,0:T(8,128)(2,1)}, u32[]{:S(2)}) copy-start(bf16[32,3072]{1,0:T(8,128)(2,1)} %param.11) | copy-start | bytes 589828
  58.2 60.5 %all-reduce.3.cloned.1.call-start = ((), (), s32[]{:S(2)}) async-start(), calls=%async_computation.2 | async-start | bytes 786432 | tf_op jit(solution)/shard_map/psum | solution.py:80
  74.7 99.3 %all-reduce.5.cloned.1.call-start = ((), (), s32[]{:S(2)}) async-start(), calls=%async_computation.3 | async-start | bytes 786432 | tf_op jit(solution)/shard_map/psum | solution.py:82
Sparse Core Ops, SparseCore 0:
  58.3 14.2 reduce-scatter.1
  75.6 42.9 all-reduce.2
  131.7 42.2 all-reduce.4
where the time goes:
time: 183 us; the launch traced here: 182 us
  waiting for transfers between devices  89.7 us (49%)
  matrix products  29.3 us (16%)
  blocking collectives  24.7 us (13%)
  other arithmetic  19.7 us (11%)
  between operations  13.9 us (8%)
  local copies, waits for them, and re-layouts  4.86 us (3%)
    psum x1, waiting for transfers between devices, layer_step(): lax.psum(jnp.dot(attn_own, w_o, preferred_element_type=jnp.float32), mode...  43.9 us
    psum x1, waiting for transfers between devices, layer_step(): lax.psum(mlp_part(hidden, g_mlp, w_gate, w_up, w_down), model_axes)  42.4 us
    pmax x1, blocking collectives, layer_step(): global_max = lax.pmax(local_max, 'kvp')  13.9 us
    select_n x1, other arithmetic, local_attention(): k_out = jnp.where(hit_mask, key_new[:, None], k_cache)  13.7 us
    psum x1, blocking collectives, layer_step(): denom_sum = lax.psum(local_sum * rescale, 'kvp')  10.7 us
    dot_general x1, matrix products, local_attention(): jnp.dot(normed, w_qkv, preferred_element_type=jnp.float32)  8.46 us
    dot_general x1, matrix products, mlp_part(): return jnp.dot(act_out, w_down, preferred_element_type=jnp.float32)  7.71 us
    dot_general x1, matrix products, local_attention(): jnp.einsum('bgrt,btgd->bgrd', prob_w.astype(jnp.bfloat16), v_out, preferr...  4.64 us
  transfers between devices with their start and end apart: 3, of which 3 were waited for; matrix products, arithmetic and copies ran while one was open for 0% of the time, Pallas kernels for 0%

commit v1 on v0

v1 whole, which is shorter than its diff:
```python
import functools

import jax
import jax.numpy as jnp
import numpy as np
from jax import lax
from jax.experimental import pallas as pl
from jax.experimental.pallas import tpu as pltpu
from jax.sharding import PartitionSpec as P

ROPE_THETA = 500000.0
EPS = 1e-5
NEG = -1e30
MESH = pl.DeviceIdType.MESH
F32 = jnp.float32
BF16 = jnp.bfloat16

B = 32
D = 3072
HD = 128
G = 4
R = 3
T = 256
HALF = D // 2
QC = 4
KC = 8
BC = B // KC
NC = 3
CW = HALF // NC
FF = 1024
SCALE = HD ** -0.5


def rms(values, gain):
    inv = lax.rsqrt(jnp.mean(values * values, axis=-1, keepdims=True) + EPS)
    return (values * inv * gain).astype(BF16)


def layer_kernel(
    ctx, freq, x_hbm, ga_hbm, gm_hbm, wq_hbm, wo_hbm, wg_hbm, wu_hbm, wd_hbm, k_hbm, v_hbm,
    kpin, vpin, knew, vnew, xout,
    x, ga, gm, wq, wo, wg, wu, wd, nbuf, acc, ang, qkv, qbuf, snbuf, obuf, mbuf, lbuf, rows, msg, cbuf,
    part1, drecv1, sum1a, recv1a, sum1b, recv1b, hbuf,
    part2, drecv2, sum2a, recv2a, sum2b, recv2b, ybuf,
    in_sem, wq_sem, kv_sem, w_sem, q_send, q_recv, c_send, c_recv,
    d_send, d_recv, a_send, a_recv, b_send, b_recv, g_send, g_recv,
):
    tp = lax.axis_index("tp")
    kvp = lax.axis_index("kvp")
    core = lax.rem(kvp, 2)
    xpos = kvp // 2
    other = 1 - core
    partner = {"kvp": xpos * 2 + other}
    first = {"tp": lax.rem(tp + core, 2), "kvp": lax.rem(xpos + 1 - core, 2) * 2 + core}
    second = {"tp": lax.rem(tp + 1 - core, 2), "kvp": lax.rem(xpos + core, 2) * 2 + core}

    def start(src, dst, sem):
        copy = pltpu.make_async_copy(src, dst, sem)
        copy.start()
        return copy

    x_in = start(x_hbm, x, in_sem.at[0])
    ga_in = start(ga_hbm, ga, in_sem.at[1])
    gm_in = start(gm_hbm, gm, in_sem.at[2])
    qrows = D // QC
    for i in range(QC):
        start(wq_hbm.at[pl.ds(i * qrows, qrows), pl.ds(pl.multiple_of(core * 1280, 128), 1280)], wq.at[i], wq_sem.at[i])
    for i in range(KC):
        start(k_hbm.at[pl.ds(i * BC, BC)], kpin.at[pl.ds(i * BC, BC)], kv_sem.at[0, i])
        start(v_hbm.at[pl.ds(i * BC, BC)], vpin.at[pl.ds(i * BC, BC)], kv_sem.at[1, i])
    wo_in = [start(wo_hbm.at[:, pl.ds(i * HALF, HALF)], wo.at[i], w_sem.at[i]) for i in range(2)]
    wg_in = start(wg_hbm, wg, w_sem.at[2])
    wu_in = start(wu_hbm, wu, w_sem.at[3])
    wd_in = [start(wd_hbm.at[:, pl.ds(i * HALF, HALF)], wd.at[i], w_sem.at[4 + i]) for i in range(2)]

    barrier = pltpu.get_barrier_semaphore()
    for step in range(1, 4):
        pl.semaphore_signal(barrier, inc=1, device_id={"kvp": lax.rem(kvp + step, 4)}, device_id_type=MESH)
    pl.semaphore_signal(barrier, inc=1, device_id={"tp": 1 - tp}, device_id_type=MESH)

    for b in range(B):
        ang[pl.ds(b, 1), :] = jnp.full((1, HD), ctx[b], jnp.int32).astype(F32) * freq[...]
    cos_t = jnp.cos(ang[...])
    lane = lax.broadcasted_iota(jnp.int32, (B, HD), 1)
    sin_t = jnp.sin(ang[...]) * jnp.where(lane < HD // 2, -1.0, 1.0)

    x_in.wait()
    ga_in.wait()
    gm_in.wait()
    nbuf[...] = rms(x[...].astype(F32), ga[...].astype(F32))

    for i in range(QC):
        pltpu.make_async_copy(wq.at[i], wq.at[i], wq_sem.at[i]).wait()
        term = jnp.dot(nbuf[:, i * qrows:(i + 1) * qrows], wq[i], preferred_element_type=F32)
        acc[...] = term if i == 0 else acc[...] + term

    def rope(values):
        return values * cos_t + pltpu.roll(values, HD // 2, 1) * sin_t

    for j in range(2):
        for r in range(R + 2):
            col = (j * (R + 2) + r) * HD
            value = acc[:, col:col + HD]
            if r <= R:
                value = rope(value)
            qkv[core, j * (R + 2) + r] = value.astype(BF16).astype(F32)

    pl.semaphore_wait(barrier, 4)
    swap = pltpu.make_async_remote_copy(
        qkv.at[core], qkv.at[core], q_send, q_recv, device_id=partner, device_id_type=MESH)
    swap.start()
    swap.wait()

    first_pos = kvp * T
    row_of = lax.broadcasted_iota(jnp.int32, (B, HD), 0)
    ctx_rows = ang
    for b in range(B):
        ctx_rows[pl.ds(b, 1), :] = jnp.full((1, HD), ctx[b] - first_pos, jnp.int32).astype(F32)
    here = (ctx_rows[...] >= 0.0) & (ctx_rows[...] < float(T))
    for g in range(G):
        base = (g % 2) * (R + 2)
        key = qkv[g // 2, base + R]
        value = qkv[g // 2, base + R + 1]
        rows[0, pl.ds(g, B, stride=G), :] = key
        rows[1, pl.ds(g, B, stride=G), :] = value
        for r in range(R):
            query = qkv[g // 2, base + r]
            qbuf[pl.ds(G * g + r, B, stride=16), :] = query
            score = jnp.sum(query * key, axis=-1, keepdims=True) * SCALE
            snbuf[pl.ds(G * g + r, B, stride=16), :] = jnp.where(here, jnp.broadcast_to(score, (B, HD)), NEG)
        qbuf[pl.ds(G * g + R, B, stride=16), :] = jnp.zeros((B, HD), F32)
        snbuf[pl.ds(G * g + R, B, stride=16), :] = jnp.full((B, HD), NEG, F32)
    knew[...] = rows[0].astype(BF16)
    vnew[...] = rows[1].astype(BF16)

    wide = (32, T * G)
    col_i = lax.broadcasted_iota(jnp.int32, wide, 1)
    row_i = lax.broadcasted_iota(jnp.int32, wide, 0)
    same_head = lax.rem(col_i, G) == lax.rem(row_i // G, G)
    row_c = lax.broadcasted_iota(jnp.int32, (32, 1), 0)

    def attend(b0):
        def pick(ref, b):
            return ref[pl.ds(pl.multiple_of(b * 16, 16), 16), :]

        q0 = pick(qbuf, b0).astype(BF16)
        q1 = pick(qbuf, b0 + 1).astype(BF16)
        zero = jnp.zeros((16, HD), BF16)
        q = jnp.concatenate(
            [jnp.concatenate([q0, zero], axis=1), jnp.concatenate([zero, q1], axis=1)], axis=0)
        k = jnp.concatenate([kpin[b0], kpin[b0 + 1]], axis=1)
        s = lax.dot_general(q, k, (((1,), (1,)), ((), ())), preferred_element_type=F32) * SCALE
        limit = jnp.where(row_c < 16, (ctx[b0] - first_pos) * G, (ctx[b0 + 1] - first_pos) * G)
        valid = same_head & (col_i < limit)
        s = jnp.where(valid, s, NEG)
        sn = jnp.concatenate([pick(snbuf, b0), pick(snbuf, b0 + 1)], axis=0)[:, :1]
        top = jnp.maximum(jnp.max(s, axis=-1, keepdims=True), sn)
        w = jnp.where(valid, jnp.exp(s - top), 0.0)
        total = jnp.sum(w, axis=-1, keepdims=True)
        v = jnp.concatenate([vpin[b0], vpin[b0 + 1]], axis=1)
        o = jnp.dot(w.astype(BF16), v, preferred_element_type=F32)
        at0 = pl.ds(pl.multiple_of(b0 * 16, 16), 16)
        at1 = pl.ds(pl.multiple_of(b0 * 16 + 16, 16), 16)
        obuf[at0, :] = o[:16, :HD]
        obuf[at1, :] = o[16:, HD:]
        both = pl.ds(pl.multiple_of(b0 * 16, 32), 32)
        mbuf[both, :] = jnp.broadcast_to(top, (32, HD))
        lbuf[both, :] = jnp.broadcast_to(total, (32, HD))

    @pl.loop(0, KC)
    def _(i):
        part = pl.ds(i * BC, BC)
        pltpu.make_async_copy(k_hbm.at[part], kpin.at[part], kv_sem.at[0, i]).wait()
        pltpu.make_async_copy(v_hbm.at[part], vpin.at[part], kv_sem.at[1, i]).wait()
        for j in range(BC // 2):
            attend(i * BC + 2 * j)

    for g in range(G):
        value = qkv[g // 2, (g % 2) * (R + 2) + R + 1]
        stats = jnp.zeros((B, HD), F32)
        for r in range(R):
            at = pl.ds(G * g + r, B, stride=16)
            top = mbuf[at, :]
            fresh = jnp.where(here, jnp.exp(snbuf[at, :] - top), 0.0)
            msg[g, r] = obuf[at, :] + fresh.astype(BF16).astype(F32) * value
            stats = jnp.where(lane == r, top, jnp.where(lane == R + r, lbuf[at, :] + fresh, stats))
        msg[g, R] = stats
    sends = []
    for step in (2, 3, 1):
        peer = lax.rem(kvp + step, 4)
        copy = pltpu.make_async_remote_copy(
            msg.at[peer], cbuf.at[step], c_send.at[step], c_recv.at[step],
            device_id={"kvp": peer}, device_id_type=MESH)
        copy.start()
        sends.append(copy)
    cbuf[0] = msg[kvp]
    for copy in sends:
        copy.wait()

    heads = []
    slots = [lax.rem(kvp - p + 4, 4) for p in range(4)]
    stats = [cbuf[s, R] for s in slots]
    for r in range(R):
        tops = [st[:, r:r + 1] for st in stats]
        top = jnp.maximum(jnp.maximum(tops[0], tops[1]), jnp.maximum(tops[2], tops[3]))
        num, den = None, None
        for s, st, t in zip(slots, stats, tops):
            f = jnp.exp(t - top)
            n_term, d_term = cbuf[s, r] * f, st[:, R + r:R + r + 1] * f
            num = n_term if num is None else num + n_term
            den = d_term if den is None else den + d_term
        heads.append((num / den).astype(BF16))
    attn = jnp.concatenate(heads, axis=1)

    def remote(src, dst, send, recv, peer):
        copy = pltpu.make_async_remote_copy(src, dst, send, recv, device_id=peer, device_id_type=MESH)
        copy.start()
        return copy

    def reduce(k, lhs, weight, part, drecv, suma, recva, sumb, recvb, out, finish):
        pend = []
        for c in range(NC):
            part[c] = jnp.dot(lhs, weight[other, :, c * CW:(c + 1) * CW], preferred_element_type=F32)
            pend.append(remote(part.at[c], drecv.at[c], d_send.at[k, c], d_recv.at[k, c], partner))
        own = [jnp.dot(lhs, weight[core, :, c * CW:(c + 1) * CW], preferred_element_type=F32) for c in range(NC)]
        last = pend
        pend = []
        for c in range(NC):
            last[c].wait()
            suma[c] = own[c] + drecv[c]
            pend.append(remote(suma.at[c], recva.at[c], a_send.at[k, c], a_recv.at[k, c], first))
        last = pend
        pend = []
        for c in range(NC):
            last[c].wait()
            sumb[c] = suma[c] + recva[c]
            pend.append(remote(sumb.at[c], recvb.at[c], b_send.at[k, c], b_recv.at[k, c], second))
        last = pend
        pend = []
        for c in range(NC):
            last[c].wait()
            out[core, c] = finish(c, sumb[c] + recvb[c])
            pend.append(remote(out.at[core, c], out.at[core, c], g_send.at[k, c], g_recv.at[k, c], partner))
        for copy in pend:
            copy.wait()

    def half_of(ref, c):
        return ref[:, pl.ds(pl.multiple_of(core * HALF + c * CW, 128), CW)]

    for copy in wo_in:
        copy.wait()
    reduce(0, attn, wo, part1, drecv1, sum1a, recv1a, sum1b, recv1b, hbuf,
           lambda c, total: (half_of(x, c).astype(F32) + total).astype(BF16).astype(F32))

    square = jnp.zeros((B, 1), F32)
    for i in range(2):
        for c in range(NC):
            square = square + jnp.sum(hbuf[i, c] * hbuf[i, c], axis=-1, keepdims=True)
    inv = lax.rsqrt(square * (1.0 / D) + EPS)
    for i in range(2):
        for c in range(NC):
            col = i * HALF + c * CW
            nbuf[:, col:col + CW] = (hbuf[i, c] * inv * gm[:, col:col + CW].astype(F32)).astype(BF16)
    wg_in.wait()
    wu_in.wait()
    acts = []
    for c in range(FF // 256):
        cols = slice(c * 256, (c + 1) * 256)
        gate = jnp.dot(nbuf[...], wg[:, cols], preferred_element_type=F32)
        up = jnp.dot(nbuf[...], wu[:, cols], preferred_element_type=F32)
        acts.append((gate * (1.0 / (1.0 + jnp.exp(-gate))) * up).astype(BF16))
    act = jnp.concatenate(acts, axis=1)
    for copy in wd_in:
        copy.wait()
    reduce(1, act, wd, part2, drecv2, sum2a, recv2a, sum2b, recv2b, ybuf,
           lambda c, total: (hbuf[core, c] + total).astype(BF16).astype(F32))
    for i in range(2):
        for c in range(NC):
            col = i * HALF + c * CW
            xout[:, col:col + CW] = ybuf[i, c].astype(BF16)


def write_kernel(ctx, k, v, knew, vnew, x, ko, vo, y, sem, row_sem):
    first_pos = lax.axis_index("kvp") * T
    pairs = ((k, knew, ko), (v, vnew, vo))

    def bulk(n, i):
        part = pl.ds(i * BC, BC)
        return pltpu.make_async_copy(pairs[n][0].at[part], pairs[n][2].at[part], sem.at[n, i])

    def row(n, b):
        pos = jnp.clip(ctx[b] - first_pos, 0, T - 1)
        return pltpu.make_async_copy(pairs[n][1].at[b], pairs[n][2].at[b, pos], row_sem)

    def held(b):
        pos = ctx[b] - first_pos
        return (pos >= 0) & (pos < T)

    x_copy = pltpu.make_async_copy(x, y, sem.at[2, 0])
    x_copy.start()
    for i in range(KC):
        for n in range(2):
            bulk(n, i).start()

    @pl.loop(0, KC)
    def _(i):
        for n in range(2):
            bulk(n, i).wait()

            @pl.loop(0, BC)
            def _(j):
                b = i * BC + j

                @pl.when(held(b))
                def _():
                    row(n, b).start()

    @pl.loop(0, B)
    def _(b):
        @pl.when(held(b))
        def _():
            row(0, b).wait()
            row(1, b).wait()

    x_copy.wait()


def solution(mesh):
    x_spec = P("dp", None)
    cache_spec = P("dp", "kvp", "tp", None)
    model_axes = ("tp", "kvp")
    inv_freq = (ROPE_THETA ** (-2.0 * np.arange(HD // 2) / HD)).astype(np.float32)
    freq = np.concatenate([inv_freq, inv_freq])[None]

    def layer_step(x_in, ctx_len, g_attn, g_mlp, w_qkv, w_o, w_gate, w_up, w_down, k_cache, v_cache):
        hbm = functools.partial(pltpu.with_memory_space_constraint, memory_space=pltpu.HBM)
        vmem = pl.BlockSpec(memory_space=pltpu.VMEM)
        anyspace = pl.BlockSpec(memory_space=pltpu.HBM)
        smem = pl.BlockSpec(memory_space=pltpu.SMEM)
        flat = (B, T * G, HD)
        chunk = pltpu.VMEM((NC, B, CW), F32)
        dma = pltpu.SemaphoreType.DMA
        kpin, vpin, knew, vnew, x_out = pl.pallas_call(
            layer_kernel,
            name="layer",
            out_shape=(
                pltpu.VMEM(flat, BF16),
                pltpu.VMEM(flat, BF16),
                pltpu.VMEM((B * G, HD), BF16),
                pltpu.VMEM((B * G, HD), BF16),
                pltpu.VMEM((B, D), BF16),
            ),
            in_specs=[smem, vmem] + [anyspace] * 10,
            out_specs=(vmem,) * 5,
            scratch_shapes=[
                pltpu.VMEM((B, D), BF16),
                pltpu.VMEM((1, D), BF16),
                pltpu.VMEM((1, D), BF16),
                pltpu.VMEM((QC, D // QC, 1280), BF16),
                pltpu.VMEM((2, 384, HALF), BF16),
                pltpu.VMEM((D, FF), BF16),
                pltpu.VMEM((D, FF), BF16),
                pltpu.VMEM((2, FF, HALF), BF16),
                pltpu.VMEM((B, D), BF16),
                pltpu.VMEM((B, 1280), F32),
                pltpu.VMEM((B, HD), F32),
                pltpu.VMEM((2, 10, B, HD), F32),
                pltpu.VMEM((B * 16, HD), F32),
                pltpu.VMEM((B * 16, HD), F32),
                pltpu.VMEM((B * 16, HD), F32),
                pltpu.VMEM((B * 16, HD), F32),
                pltpu.VMEM((B * 16, HD), F32),
                pltpu.VMEM((2, B * G, HD), F32),
                pltpu.VMEM((G, R + 1, B, HD), F32),
                pltpu.VMEM((4, R + 1, B, HD), F32),
            ]
            + ([chunk] * 6 + [pltpu.VMEM((2, NC, B, CW), F32)]) * 2
            + [dma((3,)), dma((QC,)), dma((2, KC)), dma((6,)), dma, dma, dma((4,)), dma((4,))]
            + [dma((2, NC))] * 8,
            compiler_params=pltpu.CompilerParams(
                collective_id=0, has_side_effects=True, vmem_limit_bytes=38 * 2 ** 20),
        )(
            ctx_len, freq, hbm(x_in), hbm(g_attn.reshape(1, D)), hbm(g_mlp.reshape(1, D)), hbm(w_qkv), hbm(w_o),
            hbm(w_gate), hbm(w_up), hbm(w_down), hbm(k_cache.reshape(flat)), hbm(v_cache.reshape(flat)))
        k_out, v_out, x_out = pl.pallas_call(
            write_kernel,
            name="write",
            out_shape=(
                jax.ShapeDtypeStruct(k_cache.shape, BF16),
                jax.ShapeDtypeStruct(v_cache.shape, BF16),
                jax.ShapeDtypeStruct(x_in.shape, BF16),
            ),
            in_specs=[smem] + [vmem] * 5,
            out_specs=(anyspace,) * 3,
            scratch_shapes=[dma((3, KC)), dma],
            compiler_params=pltpu.CompilerParams(vmem_limit_bytes=2 ** 20),
        )(
            ctx_len, kpin.reshape(k_cache.shape), vpin.reshape(v_cache.shape),
            knew.reshape(B, G, HD), vnew.reshape(B, G, HD), x_out)
        return x_out, k_out, v_out

    in_specs = (
        x_spec, P("dp"), P(None), P(None), P(None, "tp"), P(model_axes, None), P(None, model_axes),
        P(None, model_axes), P(model_axes, None), cache_spec, cache_spec)
    return jax.shard_map(
        layer_step, mesh=mesh, in_specs=in_specs, out_specs=(x_spec, cache_spec, cache_spec), check_vma=False)
```

time: 183 us -> 68.7 us (0.38)
  waiting for transfers between devices: 89.7 us -> 0 us
  Pallas kernels: 0 us -> 65.1 us
  matrix products: 29.3 us -> 0 us
  blocking collectives: 24.7 us -> 0 us
  other arithmetic: 19.7 us -> 0 us
  between operations: 13.9 us -> 0.65 us
  local copies, waits for them, and re-layouts: 4.86 us -> 2.6 us
    psum x2 -> x0, waiting for transfers between devices: 86.3 us -> none  [the longest x1 43.9 us: layer_step(): lax.psum(jnp.dot(attn_own, w_o, preferred_element_type=jnp.float32), mode...]
    pallas_call x0 -> x2, Pallas kernels: none -> 65.1 us  [the longest x1 58.4 us: layer_step(): pl.pallas_call(layer_kernel, name='layer', out_shape=(pltpu.VMEM(flat, BF...]
    dot_general x6 -> x0, matrix products: 29.3 us -> none  [the longest x1 8.46 us: local_attention(): jnp.dot(normed, w_qkv, preferred_element_type=jnp.float32)]
    pmax x1 -> x0, blocking collectives: 13.9 us -> none  [layer_step(): global_max = lax.pmax(local_max, 'kvp')]
    select_n x1 -> x0, other arithmetic: 13.7 us -> none  [local_attention(): k_out = jnp.where(hit_mask, key_new[:, None], k_cache)]
    psum x1 -> x0, blocking collectives: 10.7 us -> none  [layer_step(): denom_sum = lax.psum(local_sum * rescale, 'kvp')]
    unnamed x10 -> x2, local copies, waits for them, and re-layouts: 3.42 us -> 0.01 us
    reduce_scatter x1 -> x0, waiting for transfers between devices: 3.3 us -> none  [layer_step(): acc_own = lax.psum_scatter(acc_part, 'kvp', scatter_dimension=1, tiled=True)]
  transfers between devices with their start and end apart: 3 -> 0, of which waited for: 3 -> 0; matrix products, arithmetic and copies ran while one was open for 0% -> 0% of each run, Pallas kernels for 0% -> 0%
where the time goes in v1:
time: 68.7 us; the launch traced here: 68.3 us
  Pallas kernels  65.1 us (95%)
  local copies, waits for them, and re-layouts  2.6 us (4%)
    pallas_call x1, Pallas kernels, layer_step(): pl.pallas_call(layer_kernel, name='layer', out_shape=(pltpu.VMEM(flat, BF...  58.4 us
    pallas_call x1, Pallas kernels, layer_step(): pl.pallas_call(write_kernel, name='write', out_shape=(jax.ShapeDtypeStruc...  6.65 us

profile of v1, /device:TPU:0, one launch (start us, length us, event | category | flops | bytes accessed | tf_op | source)
XLA Modules:
  0.0 68.3 jit_solution(13469734745606854022)
XLA Ops:
  0.6 1.3 %reshape.30.ga_hbm = bf16[1,3072]{1,0:T(2,128)(2,1)} reshape(bf16[3072]{0:T(1024)(128)(2,1)} %param.14) | data formatting | bytes 12288 | tf_op jit(solution)/shard_map/reshape | solution.py:383
  1.9 1.3 %reshape.31.gm_hbm = bf16[1,3072]{1,0:T(2,128)(2,1)} reshape(bf16[3072]{0:T(1024)(128)(2,1)} %param.15) | data formatting | bytes 12288 | tf_op jit(solution)/shard_map/reshape | solution.py:383
  3.2 0.0 copy-start
  3.2 58.4 %layer.1 = (bf16[32,1024,128]{2,1,0:T(8,128)(2,1)S(1)}, bf16[32,1024,128]{2,1,0:T(8,128)(2,1)S(1)}, bf16[128,128]{1,0:T(8,128)(2,1)S(1)}, bf16[128,128]{1,0:T(8,128)(2,1)S(1)}, bf16[32,3072]{1,0:T(8,128)(2,1)S(1)}) custom-call(s32[32]{0:T(128)} %ctx.3, f32[1,128]{1,0:T(1,128)} %constant.2.clone.freq, bf16[32,3072]{1,0:T(8,128)(2,1)} %x_hbm.1, ...), custom_call_target="tpu_custom_call" | custom-call | tf_op jit(solution)/shard_map/layer/pallas_call | solution.py:343
  61.7 0.0 copy-done
  61.7 6.6 %write.1 = (bf16[32,256,4,128]{3,2,1,0:T(4,128)(2,1)}, bf16[32,256,4,128]{3,2,1,0:T(4,128)(2,1)}, bf16[32,3072]{1,0:T(8,128)(2,1)}) custom-call(s32[32]{0:T(128)S(1)} %copy-done, bf16[32,256,4,128]{3,2,1,0:T(4,128)(2,1)S(1)} %bitcast.6, bf16[32,256,4,128]{3,2,1,0:T(4,128)(2,1)S(1)} %bitcast.7, bf16[32,4,128]{2,1,0:T(4,128)(2,1)S(1)} %bitcast.8, ...), custom_call_target="tpu_custom_call" | custom-call | tf_op jit(solution)/shard_map/write/pallas_call | solution.py:385
Async XLA Ops:
  3.2 58.5 %copy-start = (s32[32]{0:T(128)S(1)}, s32[32]{0:T(128)}, u32[]{:S(2)}) copy-start(s32[32]{0:T(128)} %ctx.3) | copy-start | bytes 388
